TPU v7x, 256 devices: a 4x2x16 block of a 4x16x16 slice. The times are simulated.
256 devices in a mesh: groups: 2 (over y), tp: 16 (over z), tq: 4 (over x), tr: 2 (over core).
Axes of the slice: x: 4, y: 2, z: 16, core: 2. Of those that a mesh axis runs over, the one named last changes fastest.
The devices are a block of a 4x16x16 slice.
Arguments:
- attn_heads: bfloat16 [128, 16384], P('groups', ('tp', 'tq', 'tr')), parts along dimension 0, may hold values from -6 to 6
- residual: bfloat16 [128, 16384], P('groups', ('tp', 'tq', 'tr')), parts along dimension 0, may hold values from -120 to 120
- o_weight: bfloat16 [16384, 16384], P(('tp', 'tq', 'tr')), may hold values from -0.1875 to 0.1875
- norm_gain: bfloat16 [16384], P(('tp', 'tq', 'tr')), may hold values from 0.099609375 to 1.8984375
- q_weight: bfloat16 [16384, 16384], P(None, ('tp', 'tq', 'tr')), may hold values from -0.046875 to 0.046875
Outputs:
- hidden: bfloat16 [128, 16384], P('groups', ('tp', 'tq', 'tr')), parts along dimension 0
- peak_value: float32 [128], P('groups'), parts along dimension 0
- query: bfloat16 [128, 16384], P('groups', ('tp', 'tq', 'tr')), parts along dimension 0
There are 2 independent parts, one for each index of `groups`. A program takes and returns all parts, laid end to end along the dimension named above; an argument that names none is the same for every part. Nothing has to cross between parts.
All inputs are finite; a program needn't handle non-finite values. Where the computation divides by a largest or mean magnitude, that divisor is 1e-20 or more.
Results may differ from a plain program's by a relative error of at most 0.0095.
Values may be sent and summed in bfloat16 or wider, within the bound.
No kernel may reach another device: no remote copies, remote signals or barrier semaphores. Data moves between devices by JAX's collectives and lax.ppermute only.
A program may use at most 64 MiB of HBM per device.

v0:
```python
import jax
import jax.numpy as jnp
from jax import lax
from jax.sharding import PartitionSpec as P

D = 16384


def in_blocks(array, dim, devices):
    dims = array.shape
    tiles = array.reshape(*dims[:dim], devices, dims[dim] // devices, *dims[dim + 1 :])
    return jnp.moveaxis(tiles, dim, 0)


def summed_on_arrival(array, axis, dim):
    tiles = in_blocks(array, dim, lax.axis_size(axis))
    arrived = lax.all_to_all(tiles, axis, split_axis=0, concat_axis=0, tiled=True)
    return arrived.sum(axis=0)


def collected_together(array, axis):
    leaves = jax.tree.leaves(array)
    turns = sorted(range(len(leaves)), key=lambda k: -leaves[k].size)
    width = (1, *leaves[turns[0]].shape)[-1]
    lines = [
        jnp.pad(leaves[k].reshape(-1), (0, -leaves[k].size % width)).reshape(-1, width)
        for k in turns
    ]
    both, at, found = (lax.all_gather(jnp.concatenate(lines), axis), 0, {})
    for k, line in zip(turns, lines):
        share = both[:, at : at + len(line)].reshape(len(both), -1)
        found[k] = share[:, : leaves[k].size].reshape(-1, *leaves[k].shape)
        at += len(line)
    numbers = iter(range(len(leaves)))
    return jax.tree.map(lambda _: found[next(numbers)], array)


def joined_all(array, axes, combine):
    for axis in axes:
        pieces = collected_together(array, axis)
        array = jax.tree.map(lambda part: part[0], pieces)
        for k in range(1, lax.axis_size(axis)):
            array = combine(array, jax.tree.map(lambda part: part[k], pieces))
    return array


def laid_out(tiles, dim):
    tiles = jnp.moveaxis(tiles, 0, dim)
    dims = tiles.shape
    return tiles.reshape(*dims[:dim], dims[dim] * dims[dim + 1], *dims[dim + 2 :])


def from_everyone(array, axis):
    copies = jnp.broadcast_to(array, (lax.axis_size(axis), *array.shape))
    return lax.all_to_all(copies, axis, split_axis=0, concat_axis=0, tiled=True)


def collect(array, axis, dim):
    return laid_out(from_everyone(array, axis), dim)


def combine_stats(lhs_stats, rhs_stats):
    return (lhs_stats[0] + rhs_stats[0], jnp.maximum(lhs_stats[1], rhs_stats[1]))


def body(attn_heads, residual, o_weight, norm_gain, q_weight):
    terms = jnp.dot(attn_heads, o_weight, preferred_element_type=jnp.float32)
    section_one = lax.psum_scatter(terms, "tp", scatter_dimension=1, tiled=True)
    section_two = summed_on_arrival(section_one, "tq", 1)
    attn_total = summed_on_arrival(section_two, "tr", 1)
    hidden = (residual.astype(jnp.float32) + attn_total).astype(jnp.bfloat16)
    widened = hidden.astype(jnp.float32)
    gained = widened * norm_gain.astype(jnp.float32)
    squares = jnp.sum(widened * widened, axis=1)
    local_top = jnp.max(jnp.abs(gained), axis=1)
    row_total, global_top = joined_all((squares, local_top), ("tp", "tq", "tr"), combine_stats)
    inv_rms = lax.rsqrt(row_total / D + 1e-05)
    normed = gained * inv_rms[:, None]
    peak_value = global_top * inv_rms
    quantized = (normed * (448.0 / (peak_value + 1e-06))[:, None]).astype(jnp.bfloat16)
    gathered_two = collect(quantized, "tr", 1)
    gathered_four = collect(gathered_two, "tq", 1)
    projected = jnp.dot(
        lax.all_gather(gathered_four, "tp", axis=1, tiled=True),
        q_weight,
        preferred_element_type=jnp.float32,
    )
    query = (projected * ((peak_value + 1e-06) / 448.0)[:, None]).astype(jnp.bfloat16)
    return (hidden, peak_value, query)


def solution(mesh):
    placed = (
        P("groups", ("tp", "tq", "tr")),
        P("groups", ("tp", "tq", "tr")),
        P(("tp", "tq", "tr"), None),
        P(("tp", "tq", "tr")),
        P(None, ("tp", "tq", "tr")),
    )
    return jax.shard_map(
        body,
        mesh=mesh,
        in_specs=placed,
        out_specs=(P("groups", ("tp", "tq", "tr")), P("groups"), P("groups", ("tp", "tq", "tr"))),
        check_vma=False,
    )
```

profile of v0, /device:TPU:34, one launch (start us, length us, event | category | flops | bytes accessed | tf_op | source)
XLA Modules:
  0.0 252.2 jit_solution(817903353825983854)
XLA Ops:
  7.2 0.0 copy-start
  7.2 0.1 reduce-scatter.2.cloned.1.call-start
  7.3 0.6 copy-done
  7.9 4.8 %fusion.15 = f32[64,16384]{1,0:T(8,128)} fusion(bf16[64,128]{1,0:T(8,128)(2,1)S(1)} %copy-done, bf16[128,16384]{1,0:T(8,128)(2,1)} %param.7), kind=kOutput, calls=%fused_computation.64 | convolution fusion | flops 268435456 | bytes 8404992 | tf_op jit(solution)/shard_map/dot_general | solution.py:67
  12.7 0.1 reduce-scatter.2.cloned.1.call-update
  12.8 92.7 %reduce-scatter.2.cloned.1.call-done = f32[64,1024]{1,0:T(8,128)} async-done(((f32[64,16384]{1,0:T(8,128)}), f32[64,1024]{1,0:T(8,128)}) %reduce-scatter.2.cloned.1.call-update) | async-done | bytes 262160 | tf_op jit(solution)/shard_map/reduce_scatter | solution.py:68
  105.5 1.7 copy.20
  107.1 5.0 %all-to-all-start = ((f32[4,64,256]{2,1,0:T(8,128)}), f32[4,64,256]{2,1,0:T(8,128)S(1)}, u32[]{:S(2)}, u32[]{:S(2)}) async-start(f32[4,64,256]{2,1,0:T(8,128)} %bitcast.44), calls=%async_computation.1 | async-start | bytes 524288 | tf_op jit(solution)/shard_map/all_to_all | solution.py:17
  112.2 5.2 %all-to-all-done = f32[4,64,256]{2,1,0:T(8,128)S(1)} async-done(((f32[4,64,256]{2,1,0:T(8,128)}), f32[4,64,256]{2,1,0:T(8,128)S(1)}, u32[]{:S(2)}, u32[]{:S(2)}) %all-to-all-start) | async-done | bytes 262176 | tf_op jit(solution)/shard_map/all_to_all | solution.py:17
  117.5 3.8 %all_to_all.20 = f32[2,64,128]{2,1,0:T(8,128)S(1)} all-to-all(f32[2,64,128]{2,1,0:T(8,128)S(1)} %copy.12), channel_id=1, replica_groups=mesh['groups'=2,'tp'=16,'tq'=4,'tr'=2] {'tr'}, dimensions={0} | all-to-all | bytes 131072 | tf_op jit(solution)/shard_map/all_to_all | solution.py:17
  121.3 0.0 copy-done.2
  121.3 0.1 fusion.6
  121.4 0.0 copy-start.1
  121.4 27.3 %all-gather.3 = f32[16,2,64]{2,1,0:T(2,128)S(1)} all-gather(f32[1,2,64]{2,1,0:T(2,128)S(1)} %maximum_bitcast_fusion), channel_id=2, replica_groups=mesh['groups'=2,'tp'=16,'tq'=4,'tr'=2] {'tp'}, dimensions={0}, use_global_device_ids=true | all-gather | bytes 8704 | tf_op jit(solution)/shard_map/all_gather | solution.py:29
  148.7 8.5 %all-gather.4 = f32[4,2,64]{2,1,0:T(2,128)S(1)} all-gather(f32[1,2,64]{2,1,0:T(2,128)S(1)} %maximum_bitcast_fusion.1), channel_id=3, replica_groups=mesh['groups'=2,'tp'=16,'tq'=4,'tr'=2] {'tq'}, dimensions={0}, use_global_device_ids=true | all-gather | bytes 2560 | tf_op jit(solution)/shard_map/all_gather | solution.py:29
  157.3 1.9 all-gather.5
  159.1 0.0 copy-start.3
  159.2 0.1 fusion.5
  159.3 3.8 %all_to_all.21 = bf16[2,64,128]{2,1,0:T(8,128)(2,1)S(1)} all-to-all(bf16[2,64,128]{2,1,0:T(8,128)(2,1)S(1)} %broadcast_in_dim.4), channel_id=1, replica_groups=mesh['groups'=2,'tp'=16,'tq'=4,'tr'=2] {'tr'}, dimensions={0} | all-to-all | bytes 65536 | tf_op jit(solution)/shard_map/all_to_all | solution.py:55
  163.0 8.1 %all_to_all.22 = bf16[4,64,256]{2,1,0:T(8,128)(2,1)S(1)} all-to-all(bf16[4,64,256]{2,1,0:T(8,128)(2,1)S(1)} %broadcast_in_dim.5), channel_id=1, replica_groups=mesh['groups'=2,'tp'=16,'tq'=4,'tr'=2] {'tq'}, dimensions={0} | all-to-all | bytes 262144 | tf_op jit(solution)/shard_map/all_to_all | solution.py:55
  171.1 0.7 copy.17
  171.8 0.1 all-gather.8.cloned.1.call-update
  171.9 69.2 %all-gather.8.cloned.1.call-done = bf16[64,16384]{1,0:T(8,128)(2,1)} async-done(((bf16[64,1024]{1,0:T(8,128)(2,1)}), bf16[64,16384]{1,0:T(8,128)(2,1)}) %all-gather.8.cloned.1.call-update) | async-done | bytes 2097168 | tf_op jit(solution)/shard_map/all_gather | solution.py:84
  241.1 4.3 %fusion = bf16[64,128]{1,0:T(8,128)(2,1)} fusion(bf16[64,16384]{1,0:T(8,128)(2,1)} %all-gather.8.cloned.1.call-done, bf16[16384,128]{1,0:T(8,128)(2,1)} %param.9, f32[64]{0:T(128)S(1)} %get-tuple-element.5), kind=kOutput, calls=%fused_computation.1 | convolution fusion | flops 268451840 | bytes 6308096 | tf_op jit(solution)/shard_map/dot_general | solution.py:83
  (22 shorter events, 0.2 us)
Async XLA Ops:
  7.2 0.7 copy-start
  7.2 98.3 %reduce-scatter.2.cloned.1.call-start = ((), (), s32[]{:S(2)}) async-start(), calls=%async_computation.5 | async-start | bytes 4456448 | tf_op jit(solution)/shard_map/reduce_scatter | solution.py:68
  12.7 99.4 %copy-start.4 = (bf16[128]{0:T(256)(128)(2,1)S(1)}, bf16[128]{0:T(256)(128)(2,1)}, u32[]{:S(2)}) copy-start(bf16[128]{0:T(256)(128)(2,1)} %param.8) | copy-start | bytes 772
  12.7 108.5 %copy-start.2 = (bf16[64,128]{1,0:T(8,128)(2,1)S(1)}, bf16[64,128]{1,0:T(8,128)(2,1)}, u32[]{:S(2)}) copy-start(bf16[64,128]{1,0:T(8,128)(2,1)} %param.6) | copy-start | bytes 49156
  107.1 10.3 %all-to-all-start = ((f32[4,64,256]{2,1,0:T(8,128)}), f32[4,64,256]{2,1,0:T(8,128)S(1)}, u32[]{:S(2)}, u32[]{:S(2)}) async-start(f32[4,64,256]{2,1,0:T(8,128)} %bitcast.44), calls=%async_computation.1 | async-start | bytes 524288 | tf_op jit(solution)/shard_map/all_to_all | solution.py:17
  112.2 128.9 %all-gather.8.cloned.1.call-start = ((), (), s32[]{:S(2)}) async-start(), calls=%async_computation.6 | async-start | bytes 2228224 | tf_op jit(solution)/shard_map/all_gather | solution.py:84
  121.4 124.0 %copy-start.1 = (bf16[64,128]{1,0:T(8,128)(2,1)}, bf16[64,128]{1,0:T(8,128)(2,1)S(1)}, u32[]{:S(2)}) copy-start(bf16[64,128]{1,0:T(8,128)(2,1)S(1)} %get-tuple-element.8) | copy-start | bytes 49156
  159.1 86.2 %copy-start.3 = (f32[64]{0:T(128)}, f32[64]{0:T(128)S(1)}, u32[]{:S(2)}) copy-start(f32[64]{0:T(128)S(1)} %get-tuple-element.6) | copy-start | bytes 772
Sparse Core Ops, SparseCore 0:
  12.9 92.5 reduce-scatter.1
  172.0 69.0 all-gather.7
where the time goes:
time: 253 us; the launch traced here: 252 us
  waiting for transfers between devices  167 us (66%)
  blocking collectives  53.3 us (21%)
  between operations  14.2 us (6%)
  matrix products  9.1 us (4%)
  starting transfers between devices  5.09 us (2%)
  local copies, waits for them, and re-layouts  3.06 us (1%)
    reduce_scatter x1, waiting for transfers between devices, body(): section_one = lax.psum_scatter(terms, 'tp', scatter_dimension=1, tiled=True)  92.7 us
    all_gather x1, waiting for transfers between devices, body(): lax.all_gather(gathered_four, 'tp', axis=1, tiled=True)  69.2 us
    all_gather x3, blocking collectives, collected_together(): both, at, found = (lax.all_gather(jnp.concatenate(lines), axis), 0, {})  37.6 us
    all_to_all x2, blocking collectives, from_everyone(): return lax.all_to_all(copies, axis, split_axis=0, concat_axis=0, tiled=True)  11.9 us
    all_to_all x1, waiting for transfers between devices, summed_on_arrival(): lax.all_to_all(tiles, axis, split_axis=0, concat_axis=0, tiled=True)  5.21 us
  transfers between devices with their start and end apart: 3, of which 3 were waited for; matrix products, arithmetic and copies ran while one was open for 0% of the time, Pallas kernels for 0%

commit v1 on v0

--- a/solution.py
+++ b/solution.py
@@ -1,9 +1,20 @@
+import functools
 import jax
 import jax.numpy as jnp
 from jax import lax
 from jax.sharding import PartitionSpec as P
 
 D = 16384
+
+
+def get_the_forms(matrix, along_axis):
+    front = lax.axis_size(along_axis)
+    wide_out = jnp.stack(front * [matrix], axis=0)
+    state_next = lax.all_to_all(wide_out, along_axis, split_axis=0, concat_axis=0)
+    return jnp.concatenate(state_next, axis=1)
+
+
+handle_kinds_for = functools.partial(get_the_forms, along_axis="tp")
 
 
 def in_blocks(array, dim, devices):
@@ -81,9 +92,7 @@
     gathered_two = collect(quantized, "tr", 1)
     gathered_four = collect(gathered_two, "tq", 1)
     projected = jnp.dot(
-        lax.all_gather(gathered_four, "tp", axis=1, tiled=True),
-        q_weight,
-        preferred_element_type=jnp.float32,
+        handle_kinds_for(gathered_four), q_weight, preferred_element_type=jnp.float32
     )
     query = (projected * ((peak_value + 1e-06) / 448.0)[:, None]).astype(jnp.bfloat16)
     return (hidden, peak_value, query)

time: 253 us -> 286 us (1.13)
  blocking collectives: 53.3 us -> 159 us
  waiting for transfers between devices: 167 us -> 97.9 us
    all_to_all x0 -> x1, blocking collectives: none -> 106 us  [get_the_forms(): lax.all_to_all(wide_out, along_axis, split_axis=0, concat_axis=0)]
    all_gather x1 -> x0, waiting for transfers between devices: 69.2 us -> none  [body(): lax.all_gather(gathered_four, 'tp', axis=1, tiled=True)]
  transfers between devices with their start and end apart: 3 -> 2, of which waited for: 3 -> 2; matrix products, arithmetic and copies ran while one was open for 0% -> 0% of each run, Pallas kernels for 0% -> 0%
where the time goes in v1:
time: 286 us
  blocking collectives  159 us (56%)
  waiting for transfers between devices  97.9 us (34%)
  between operations  14.2 us (5%)
  matrix products  6.28 us (2%)
  starting transfers between devices  5.09 us (2%)
  local copies, waits for them, and re-layouts  2.9 us (1%)
    all_to_all x1, blocking collectives, get_the_forms(): lax.all_to_all(wide_out, along_axis, split_axis=0, concat_axis=0)  106 us
    reduce_scatter x1, waiting for transfers between devices, body(): section_one = lax.psum_scatter(terms, 'tp', scatter_dimension=1, tiled=True)  92.7 us
    all_gather x3, blocking collectives, collected_together(): both, at, found = (lax.all_gather(jnp.concatenate(lines), axis), 0, {})  37.6 us
    all_to_all x2, blocking collectives, from_everyone(): return lax.all_to_all(copies, axis, split_axis=0, concat_axis=0, tiled=True)  11.9 us
  transfers between devices with their start and end apart: 2, of which 2 were waited for; matrix products, arithmetic and copies ran while one was open for 0% of the time, Pallas kernels for 0%

profile of v1, /device:TPU:34, one launch (start us, length us, event | category | flops | bytes accessed | tf_op | source)
XLA Modules:
  0.0 285.6 jit_solution(1174764520111062832)
XLA Ops:
  7.2 0.0 copy-start
  7.2 0.1 reduce-scatter.2.cloned.1.call-start
  7.3 0.6 copy-done
  7.9 4.8 %fusion.15 = f32[64,16384]{1,0:T(8,128)} fusion(bf16[64,128]{1,0:T(8,128)(2,1)S(1)} %copy-done, bf16[128,16384]{1,0:T(8,128)(2,1)} %param.7), kind=kOutput, calls=%fused_computation.64 | convolution fusion | flops 268435456 | bytes 8404992 | tf_op jit(solution)/shard_map/dot_general | solution.py:78
  12.7 0.1 reduce-scatter.2.cloned.1.call-update
  12.8 92.7 %reduce-scatter.2.cloned.1.call-done = f32[64,1024]{1,0:T(8,128)} async-done(((f32[64,16384]{1,0:T(8,128)}), f32[64,1024]{1,0:T(8,128)}) %reduce-scatter.2.cloned.1.call-update) | async-done | bytes 262160 | tf_op jit(solution)/shard_map/reduce_scatter | solution.py:79
  105.5 1.7 copy.23
  107.1 5.0 %all-to-all-start = ((f32[4,64,256]{2,1,0:T(8,128)}), f32[4,64,256]{2,1,0:T(8,128)S(1)}, u32[]{:S(2)}, u32[]{:S(2)}) async-start(f32[4,64,256]{2,1,0:T(8,128)} %bitcast.47), calls=%async_computation.1 | async-start | bytes 524288 | tf_op jit(solution)/shard_map/all_to_all | solution.py:28
  112.2 5.2 %all-to-all-done = f32[4,64,256]{2,1,0:T(8,128)S(1)} async-done(((f32[4,64,256]{2,1,0:T(8,128)}), f32[4,64,256]{2,1,0:T(8,128)S(1)}, u32[]{:S(2)}, u32[]{:S(2)}) %all-to-all-start) | async-done | bytes 262176 | tf_op jit(solution)/shard_map/all_to_all | solution.py:28
  117.4 3.8 %all_to_all.25 = f32[2,64,128]{2,1,0:T(8,128)S(1)} all-to-all(f32[2,64,128]{2,1,0:T(8,128)S(1)} %copy.13), channel_id=1, replica_groups=mesh['groups'=2,'tp'=16,'tq'=4,'tr'=2] {'tr'}, dimensions={0} | all-to-all | bytes 131072 | tf_op jit(solution)/shard_map/all_to_all | solution.py:28
  121.3 0.1 fusion.6
  121.4 0.0 copy-start.2
  121.4 27.3 %all-gather.3 = f32[16,2,64]{2,1,0:T(2,128)S(1)} all-gather(f32[1,2,64]{2,1,0:T(2,128)S(1)} %maximum_bitcast_fusion), channel_id=2, replica_groups=mesh['groups'=2,'tp'=16,'tq'=4,'tr'=2] {'tp'}, dimensions={0}, use_global_device_ids=true | all-gather | bytes 8704 | tf_op jit(solution)/shard_map/all_gather | solution.py:40
  148.7 8.5 %all-gather.4 = f32[4,2,64]{2,1,0:T(2,128)S(1)} all-gather(f32[1,2,64]{2,1,0:T(2,128)S(1)} %maximum_bitcast_fusion.1), channel_id=3, replica_groups=mesh['groups'=2,'tp'=16,'tq'=4,'tr'=2] {'tq'}, dimensions={0}, use_global_device_ids=true | all-gather | bytes 2560 | tf_op jit(solution)/shard_map/all_gather | solution.py:40
  157.3 1.9 all-gather.5
  159.1 0.0 copy-start.4
  159.1 0.1 fusion.5
  159.2 3.8 %all_to_all.26 = bf16[2,64,128]{2,1,0:T(8,128)(2,1)S(1)} all-to-all(bf16[2,64,128]{2,1,0:T(8,128)(2,1)S(1)} %broadcast_in_dim.4), channel_id=1, replica_groups=mesh['groups'=2,'tp'=16,'tq'=4,'tr'=2] {'tr'}, dimensions={0} | all-to-all | bytes 65536 | tf_op jit(solution)/shard_map/all_to_all | solution.py:66
  163.0 8.1 %all_to_all.27 = bf16[4,64,256]{2,1,0:T(8,128)(2,1)S(1)} all-to-all(bf16[4,64,256]{2,1,0:T(8,128)(2,1)S(1)} %broadcast_in_dim.5), channel_id=1, replica_groups=mesh['groups'=2,'tp'=16,'tq'=4,'tr'=2] {'tq'}, dimensions={0} | all-to-all | bytes 262144 | tf_op jit(solution)/shard_map/all_to_all | solution.py:66
  171.1 0.3 stack.3
  171.4 0.0 copy-start.1
  171.4 105.6 %all_to_all.28 = bf16[16,64,1024]{2,1,0:T(8,128)(2,1)S(1)} all-to-all(bf16[16,64,1024]{2,1,0:T(8,128)(2,1)S(1)} %stack.3), channel_id=1, replica_groups=mesh['groups'=2,'tp'=16,'tq'=4,'tr'=2] {'tp'}, dimensions={0} | all-to-all | bytes 4194304 | tf_op jit(solution)/shard_map/all_to_all | solution.py:13
  277.0 0.2 copy.20
  277.3 1.5 fusion
  (24 shorter events, 0.2 us)
Async XLA Ops:
  7.2 0.7 copy-start
  7.2 98.3 %reduce-scatter.2.cloned.1.call-start = ((), (), s32[]{:S(2)}) async-start(), calls=%async_computation.6 | async-start | bytes 4456448 | tf_op jit(solution)/shard_map/reduce_scatter | solution.py:79
  12.7 99.4 %copy-start.5 = (bf16[128]{0:T(256)(128)(2,1)S(1)}, bf16[128]{0:T(256)(128)(2,1)}, u32[]{:S(2)}) copy-start(bf16[128]{0:T(256)(128)(2,1)} %param.8) | copy-start | bytes 772
  12.7 108.5 %copy-start.3 = (bf16[64,128]{1,0:T(8,128)(2,1)S(1)}, bf16[64,128]{1,0:T(8,128)(2,1)}, u32[]{:S(2)}) copy-start(bf16[64,128]{1,0:T(8,128)(2,1)} %param.6) | copy-start | bytes 49156
  107.1 10.3 %all-to-all-start = ((f32[4,64,256]{2,1,0:T(8,128)}), f32[4,64,256]{2,1,0:T(8,128)S(1)}, u32[]{:S(2)}, u32[]{:S(2)}) async-start(f32[4,64,256]{2,1,0:T(8,128)} %bitcast.47), calls=%async_computation.1 | async-start | bytes 524288 | tf_op jit(solution)/shard_map/all_to_all | solution.py:28
  121.4 155.9 %copy-start.2 = (bf16[64,128]{1,0:T(8,128)(2,1)}, bf16[64,128]{1,0:T(8,128)(2,1)S(1)}, u32[]{:S(2)}) copy-start(bf16[64,128]{1,0:T(8,128)(2,1)S(1)} %get-tuple-element.8) | copy-start | bytes 49156
  159.1 118.1 %copy-start.4 = (f32[64]{0:T(128)}, f32[64]{0:T(128)S(1)}, u32[]{:S(2)}) copy-start(f32[64]{0:T(128)S(1)} %get-tuple-element.6) | copy-start | bytes 772
  171.4 105.9 %copy-start.1 = (bf16[16384,128]{1,0:T(8,128)(2,1)S(1)}, bf16[16384,128]{1,0:T(8,128)(2,1)}, u32[]{:S(2)}) copy-start(bf16[16384,128]{1,0:T(8,128)(2,1)} %param.9) | copy-start | bytes 12582916
Sparse Core Ops, SparseCore 0:
  12.9 92.5 reduce-scatter.1
